TPU v7x, 32 devices: a whole 2x2x4 slice. The times are simulated.
32 devices in a mesh: tensor: 4 (over x, core), dp: 4 (over z), ctx: 2 (over y).
Axes of the slice: x: 2, y: 2, z: 4, core: 2. Of those that a mesh axis runs over, the one named last changes fastest.
Arguments:
- inputs: bfloat16 [4, 1024, 2048], P('dp', 'ctx'), may hold values from -8 to 8
- cotangent: bfloat16 [4, 1024, 2048], P('dp', 'ctx'), may hold values from -6 to 6
- qkv_state: float32 [3, 2, 2048, 3, 2048], P(None, None, ('dp', 'ctx'), None, 'tensor'), may hold values from -1024 to 1024, as said below
- out_state: float32 [3, 2, 2048, 2048], P(None, None, 'tensor', ('dp', 'ctx')), may hold values from -1024 to 1024, as said below
- up_state: float32 [3, 2, 2048, 8192], P(None, None, ('dp', 'ctx'), 'tensor'), may hold values from -1024 to 1024, as said below
- down_state: float32 [3, 2, 8192, 2048], P(None, None, 'tensor', ('dp', 'ctx')), may hold values from -1024 to 1024, as said below
- qkv_bias_state: float32 [3, 2, 3, 2048], P(None, None, None, ('tensor', 'dp', 'ctx')), may hold values from -1024 to 1024, as said below
- up_bias_state: float32 [3, 2, 8192], P(None, None, ('tensor', 'dp', 'ctx')), may hold values from -1024 to 1024, as said below
- norm_state: float32 [3, 2, 5, 2048], P(None, None, None, ('dp', 'ctx')), may hold values from -1024 to 1024, as said below
Outputs:
- outputs: bfloat16 [4, 1024, 2048], P('dp', 'ctx')
- input_grad: float32 [4, 1024, 2048], P('dp', 'ctx')
- qkv_grad: float32 [3, 2, 2048, 3, 2048], P(None, None, ('dp', 'ctx'), None, 'tensor')
- qkv_new: float32 [2, 2048, 3, 2048], P(None, ('dp', 'ctx'), None, 'tensor')
- out_grad: float32 [3, 2, 2048, 2048], P(None, None, 'tensor', ('dp', 'ctx'))
- out_new: float32 [2, 2048, 2048], P(None, 'tensor', ('dp', 'ctx'))
- up_grad: float32 [3, 2, 2048, 8192], P(None, None, ('dp', 'ctx'), 'tensor')
- up_new: float32 [2, 2048, 8192], P(None, ('dp', 'ctx'), 'tensor')
- down_grad: float32 [3, 2, 8192, 2048], P(None, None, 'tensor', ('dp', 'ctx'))
- down_new: float32 [2, 8192, 2048], P(None, 'tensor', ('dp', 'ctx'))
- qkv_bias_grad: float32 [3, 2, 3, 2048], P(None, None, None, ('tensor', 'dp', 'ctx'))
- qkv_bias_new: float32 [2, 3, 2048], P(None, None, ('tensor', 'dp', 'ctx'))
- up_bias_grad: float32 [3, 2, 8192], P(None, None, ('tensor', 'dp', 'ctx'))
- up_bias_new: float32 [2, 8192], P(None, ('tensor', 'dp', 'ctx'))
- norm_grad: float32 [3, 2, 5, 2048], P(None, None, None, ('dp', 'ctx'))
- norm_new: float32 [2, 5, 2048], P(None, None, ('dp', 'ctx'))
Inputs may be any that keep to these rules, and one draw needn't show every extreme that they name: `qkv_state`: index 0 of the first dimension holds the weights, 1 the first moments, 2 the roots of the second moments, which are positive. `out_state`: index 0 of the first dimension holds the weights, 1 the first moments, 2 the roots of the second moments, which are positive. `up_state`: index 0 of the first dimension holds the weights, 1 the first moments, 2 the roots of the second moments, which are positive. `down_state`: index 0 of the first dimension holds the weights, 1 the first moments, 2 the roots of the second moments, which are positive. `qkv_bias_state`: index 0 of the first dimension holds the biases, 1 the first moments, 2 the roots of the second moments, which are positive. `up_bias_state`: index 0 of the first dimension holds the biases, 1 the first moments, 2 the roots of the second moments, which are positive. `norm_state`: index 0 of the first dimension holds the gains, shifts and output bias, 1 the first moments, 2 the roots of the second moments, which are positive.
All inputs are finite; a program needn't handle non-finite values.
Results may differ from a plain program's by a relative error of at most 0.015.
Values may be sent and summed in bfloat16 or wider, within the bound.
A program may use at most 384 MiB of HBM per device.

v0:
```python
import jax
import jax.numpy as jnp
from jax import lax
from jax.sharding import PartitionSpec as P

HEAD_DIM = 256
ROT = 64
STEP = 4
beta_one = 0.9
beta_two = 0.95
adam_eps = 1e-08
norm_eps = 1e-05
rate_matrix = 0.008
rate_vector = 0.2
weight_decay = 0.01


def layer_norm(values, norm_gain, norm_shift):
    centered = values - jnp.mean(values, axis=-1, keepdims=True)
    spread = jnp.mean(centered * centered, axis=-1, keepdims=True)
    return centered * lax.rsqrt(spread + norm_eps) * norm_gain + norm_shift


def angle_tables(positions, rotated):
    halfway = rotated // 2
    frequency = 10000.0 ** (-2.0 * jnp.arange(halfway, dtype=jnp.float32) / rotated)
    angles = positions[:, None] * frequency[None, :]
    return (jnp.cos(angles)[:, None, :], jnp.sin(angles)[:, None, :])


def rotate(features_in, cosine_table, sine_table):
    halfway = cosine_table.shape[-1]
    lower_half = features_in[..., :halfway]
    upper_half = features_in[..., halfway : 2 * halfway]
    return jnp.concatenate(
        [
            lower_half * cosine_table - upper_half * sine_table,
            upper_half * cosine_table + lower_half * sine_table,
            features_in[..., 2 * halfway :],
        ],
        axis=-1,
    )


def rotate_back(features_in, cosine_table, sine_table):
    halfway = cosine_table.shape[-1]
    lower_half = features_in[..., :halfway]
    upper_half = features_in[..., halfway : 2 * halfway]
    return jnp.concatenate(
        [
            lower_half * cosine_table + upper_half * sine_table,
            upper_half * cosine_table - lower_half * sine_table,
            features_in[..., 2 * halfway :],
        ],
        axis=-1,
    )


def adam_step(packed, gradient, learn_rate, decay_rate):
    moment = beta_one * packed[1] + (1.0 - beta_one) * gradient
    root_second = jnp.sqrt(
        beta_two * packed[2] * packed[2] + (1.0 - beta_two) * gradient * gradient
    )
    update = (
        learn_rate
        * (moment / (1.0 - beta_one**STEP))
        / (root_second / (1.0 - beta_two**STEP) ** 0.5 + adam_eps)
    )
    weight = packed[0] - update - learn_rate * decay_rate * packed[0]
    return (jnp.stack([gradient, moment, root_second]), weight)


def lowered(packed, layer_index):
    return packed[0, layer_index].astype(jnp.bfloat16)


def causal_scores(queries, key_block, ctx_place):
    row_span = queries.shape[1]
    length = key_block.shape[1]
    scores = jnp.einsum(
        "sqhd,skhd->shqk", queries, key_block, preferred_element_type=jnp.float32
    ) * HEAD_DIM ** (-0.5)
    query_pos = ctx_place * row_span + jnp.arange(row_span, dtype=jnp.int32)
    causal = jnp.arange(length, dtype=jnp.int32)[None, :] <= query_pos[:, None]
    return jnp.where(causal[None, None], scores, -1e30)


def forward_layer(hidden, weights, cosine_table, sine_table, ctx_place):
    qkv_weight, out_weight, up_weight, down_weight, bias_triple, up_bias, norm_rows = weights
    bias_full = bias_triple.astype(jnp.float32)
    norm_rows = norm_rows.astype(jnp.float32)
    sequences, row_span, features = hidden.shape
    local_width = qkv_weight.shape[2]
    head_count = local_width // HEAD_DIM
    normed_one = layer_norm(hidden, norm_rows[0], norm_rows[1]).astype(jnp.bfloat16)
    normed_two = layer_norm(hidden, norm_rows[2], norm_rows[3]).astype(jnp.bfloat16)
    projected = (
        jnp.einsum("scd,dkj->sckj", normed_one, qkv_weight, preferred_element_type=jnp.float32)
        + bias_full
    )
    projected = projected.reshape(sequences, row_span, 3, head_count, HEAD_DIM)
    queries = rotate(projected[:, :, 0], cosine_table, sine_table).astype(jnp.bfloat16)
    keys_here = rotate(projected[:, :, 1], cosine_table, sine_table).astype(jnp.bfloat16)
    values_here = projected[:, :, 2].astype(jnp.bfloat16)
    key_block, value_block = (
        lax.all_gather(keys_here, "ctx", axis=1, tiled=True),
        lax.all_gather(values_here, "ctx", axis=1, tiled=True),
    )
    scores = causal_scores(queries, key_block, ctx_place)
    row_peak = jnp.max(scores, axis=-1, keepdims=True)
    exponent = jnp.exp(scores - row_peak)
    row_total = jnp.sum(exponent, axis=-1, keepdims=True)
    attention = exponent / row_total
    log_total = row_peak + jnp.log(row_total)
    mixture = jnp.einsum(
        "shqk,skhd->sqhd",
        attention.astype(jnp.bfloat16),
        value_block,
        preferred_element_type=jnp.float32,
    )
    mixture = mixture.reshape(sequences, row_span, local_width).astype(jnp.bfloat16)
    pre_act = jnp.einsum(
        "scd,df->scf", normed_two, up_weight, preferred_element_type=jnp.float32
    ) + up_bias.astype(jnp.float32)
    activation = jax.nn.gelu(pre_act, approximate=False).astype(jnp.bfloat16)
    summand = jnp.einsum("scj,jd->scd", mixture, out_weight, preferred_element_type=jnp.float32)
    summand = summand + jnp.einsum(
        "scf,fd->scd", activation, down_weight, preferred_element_type=jnp.float32
    )
    branch = lax.psum(summand, "tensor")
    saved = (
        hidden,
        normed_one,
        normed_two,
        queries,
        key_block,
        value_block,
        log_total,
        mixture,
        pre_act,
        activation,
    )
    return (hidden + branch + norm_rows[4], saved)


def backward_layer(gradient, weights, stored, cosine_table, sine_table, ctx_place):
    qkv_weight, out_weight, up_weight, down_weight, bias_triple, up_bias, norm_rows = weights
    norm_rows = norm_rows.astype(jnp.float32)
    (
        hidden,
        normed_one,
        normed_two,
        queries,
        key_block,
        value_block,
        log_total,
        mixture,
        pre_act,
        activation,
    ) = stored
    sequences, row_span, features = gradient.shape
    local_width = qkv_weight.shape[2]
    head_count = local_width // HEAD_DIM
    grad_low = gradient.astype(jnp.bfloat16)
    grad_bias_sum = jnp.sum(gradient, axis=(0, 1))
    grad_out_w = jnp.einsum("scj,scd->jd", mixture, grad_low, preferred_element_type=jnp.float32)
    grad_down_w = jnp.einsum(
        "scf,scd->fd", activation, grad_low, preferred_element_type=jnp.float32
    )
    grad_mixture = jnp.einsum(
        "scd,jd->scj", grad_low, out_weight, preferred_element_type=jnp.float32
    ).astype(jnp.bfloat16)
    grad_activation = jnp.einsum(
        "scd,fd->scf", grad_low, down_weight, preferred_element_type=jnp.float32
    )
    unused_value, gelu_back = jax.vjp(
        lambda argument: jax.nn.gelu(argument, approximate=False), pre_act
    )
    grad_pre = gelu_back(grad_activation)[0].astype(jnp.bfloat16)
    grad_up_bias = jnp.sum(grad_pre.astype(jnp.float32), axis=(0, 1))
    grad_up_w = jnp.einsum("scd,scf->df", normed_two, grad_pre, preferred_element_type=jnp.float32)
    grad_normed_two = jnp.einsum(
        "scf,df->scd", grad_pre, up_weight, preferred_element_type=jnp.float32
    )
    grad_heads = grad_mixture.reshape(sequences, row_span, head_count, HEAD_DIM)
    scores = causal_scores(queries, key_block, ctx_place)
    attention = jnp.exp(scores - log_total)
    grad_attention = jnp.einsum(
        "sqhd,skhd->shqk", grad_heads, value_block, preferred_element_type=jnp.float32
    )
    row_delta = jnp.sum(attention * grad_attention, axis=-1, keepdims=True)
    grad_scores = (attention * (grad_attention - row_delta)).astype(jnp.bfloat16)
    score_scale = HEAD_DIM ** (-0.5)
    grad_queries = (
        jnp.einsum("shqk,skhd->sqhd", grad_scores, key_block, preferred_element_type=jnp.float32)
        * score_scale
    )
    key_terms = (
        jnp.einsum("shqk,sqhd->skhd", grad_scores, queries, preferred_element_type=jnp.float32)
        * score_scale
    )
    value_terms = jnp.einsum(
        "shqk,sqhd->skhd",
        attention.astype(jnp.bfloat16),
        grad_heads,
        preferred_element_type=jnp.float32,
    )
    grad_keys, grad_values = (
        lax.psum_scatter(
            key_terms.astype(jnp.bfloat16), "ctx", scatter_dimension=1, tiled=True
        ).astype(jnp.float32),
        lax.psum_scatter(
            value_terms.astype(jnp.bfloat16), "ctx", scatter_dimension=1, tiled=True
        ).astype(jnp.float32),
    )
    grad_projected = jnp.stack(
        [
            rotate_back(grad_queries, cosine_table, sine_table),
            rotate_back(grad_keys, cosine_table, sine_table),
            grad_values,
        ],
        axis=2,
    )
    grad_projected = grad_projected.reshape(sequences, row_span, 3, local_width).astype(
        jnp.bfloat16
    )
    grad_qkv_bias = jnp.sum(grad_projected.astype(jnp.float32), axis=(0, 1))
    grad_qkv_w = jnp.einsum(
        "scd,sckj->dkj", normed_one, grad_projected, preferred_element_type=jnp.float32
    )
    grad_normed_one = jnp.einsum(
        "sckj,dkj->scd", grad_projected, qkv_weight, preferred_element_type=jnp.float32
    )
    grad_normed_one, grad_normed_two = (
        lax.psum(grad_normed_one.astype(jnp.bfloat16), "tensor").astype(jnp.float32),
        lax.psum(grad_normed_two.astype(jnp.bfloat16), "tensor").astype(jnp.float32),
    )
    unused_one, norm_back_one = jax.vjp(layer_norm, hidden, norm_rows[0], norm_rows[1])
    unused_two, norm_back_two = jax.vjp(layer_norm, hidden, norm_rows[2], norm_rows[3])
    hidden_one, gain_one, shift_one = norm_back_one(grad_normed_one)
    hidden_two, gain_two, shift_two = norm_back_two(grad_normed_two)
    grad_vectors = jnp.stack([gain_one, shift_one, gain_two, shift_two, grad_bias_sum])
    pieces = (
        grad_qkv_w,
        grad_out_w,
        grad_up_w,
        grad_down_w,
        grad_qkv_bias,
        grad_up_bias,
        grad_vectors,
    )
    return (gradient + hidden_one + hidden_two, pieces)


def stack_member(collected, member):
    return jnp.stack([collected[layer_index][member] for layer_index in range(len(collected))])


def local(
    inputs,
    cotangent,
    qkv_state,
    out_state,
    up_state,
    down_state,
    qkv_bias_state,
    up_bias_state,
    norm_state,
):
    layers = qkv_state.shape[1]
    sequences, row_span, features = inputs.shape
    ctx_place = lax.axis_index("ctx")
    positions = (ctx_place * row_span + jnp.arange(row_span, dtype=jnp.int32)).astype(jnp.float32)
    cosine_table, sine_table = angle_tables(positions, ROT)
    hidden = inputs.astype(jnp.float32)
    fetched = []
    stored = []
    for layer_index in range(layers):
        weights = (
            lax.all_gather(lowered(qkv_state, layer_index), ("dp", "ctx"), axis=0, tiled=True),
            lax.all_gather(lowered(out_state, layer_index), ("dp", "ctx"), axis=1, tiled=True),
            lax.all_gather(lowered(up_state, layer_index), ("dp", "ctx"), axis=0, tiled=True),
            lax.all_gather(lowered(down_state, layer_index), ("dp", "ctx"), axis=1, tiled=True),
            lax.all_gather(lowered(qkv_bias_state, layer_index), ("dp", "ctx"), axis=1, tiled=True),
            lax.all_gather(lowered(up_bias_state, layer_index), ("dp", "ctx"), axis=0, tiled=True),
            lax.all_gather(lowered(norm_state, layer_index), ("dp", "ctx"), axis=1, tiled=True),
        )
        hidden, saved = forward_layer(hidden, weights, cosine_table, sine_table, ctx_place)
        fetched.append(weights)
        stored.append(saved)
    outputs = hidden.astype(jnp.bfloat16)
    gradient = cotangent.astype(jnp.float32)
    collected = [None] * layers
    for layer_index in reversed(range(layers)):
        weights = (
            lax.all_gather(lowered(qkv_state, layer_index), ("dp", "ctx"), axis=0, tiled=True),
            lax.all_gather(lowered(out_state, layer_index), ("dp", "ctx"), axis=1, tiled=True),
            lax.all_gather(lowered(up_state, layer_index), ("dp", "ctx"), axis=0, tiled=True),
            lax.all_gather(lowered(down_state, layer_index), ("dp", "ctx"), axis=1, tiled=True),
            lax.all_gather(lowered(qkv_bias_state, layer_index), ("dp", "ctx"), axis=1, tiled=True),
            lax.all_gather(lowered(up_bias_state, layer_index), ("dp", "ctx"), axis=0, tiled=True),
            lax.all_gather(lowered(norm_state, layer_index), ("dp", "ctx"), axis=1, tiled=True),
        )
        gradient, pieces = backward_layer(
            gradient, weights, stored[layer_index], cosine_table, sine_table, ctx_place
        )
        collected[layer_index] = pieces
    totals = (
        lax.psum_scatter(
            stack_member(collected, 0).astype(jnp.bfloat16),
            ("dp", "ctx"),
            scatter_dimension=1,
            tiled=True,
        ).astype(jnp.float32),
        lax.psum_scatter(
            stack_member(collected, 1).astype(jnp.bfloat16),
            ("dp", "ctx"),
            scatter_dimension=2,
            tiled=True,
        ).astype(jnp.float32),
        lax.psum_scatter(
            stack_member(collected, 2).astype(jnp.bfloat16),
            ("dp", "ctx"),
            scatter_dimension=1,
            tiled=True,
        ).astype(jnp.float32),
        lax.psum_scatter(
            stack_member(collected, 3).astype(jnp.bfloat16),
            ("dp", "ctx"),
            scatter_dimension=2,
            tiled=True,
        ).astype(jnp.float32),
        lax.psum_scatter(
            stack_member(collected, 4).astype(jnp.bfloat16),
            ("dp", "ctx"),
            scatter_dimension=2,
            tiled=True,
        ).astype(jnp.float32),
        lax.psum_scatter(
            stack_member(collected, 5).astype(jnp.bfloat16),
            ("dp", "ctx"),
            scatter_dimension=1,
            tiled=True,
        ).astype(jnp.float32),
        lax.psum_scatter(
            stack_member(collected, 6).astype(jnp.bfloat16),
            ("dp", "ctx"),
            scatter_dimension=2,
            tiled=True,
        ).astype(jnp.float32),
    )
    qkv_pack, qkv_new = adam_step(qkv_state, totals[0], rate_matrix, weight_decay)
    out_pack, out_new = adam_step(out_state, totals[1], rate_matrix, weight_decay)
    up_pack, up_new = adam_step(up_state, totals[2], rate_matrix, weight_decay)
    down_pack, down_new = adam_step(down_state, totals[3], rate_matrix, weight_decay)
    qkv_bias_pack, qkv_bias_new = adam_step(qkv_bias_state, totals[4], rate_vector, 0.0)
    up_bias_pack, up_bias_new = adam_step(up_bias_state, totals[5], rate_vector, 0.0)
    norm_pack, norm_new = adam_step(norm_state, totals[6], rate_vector, 0.0)
    return (
        outputs,
        gradient,
        qkv_pack,
        qkv_new,
        out_pack,
        out_new,
        up_pack,
        up_new,
        down_pack,
        down_new,
        qkv_bias_pack,
        qkv_bias_new,
        up_bias_pack,
        up_bias_new,
        norm_pack,
        norm_new,
    )


def solution(mesh):
    return jax.shard_map(
        local,
        mesh=mesh,
        in_specs=(
            P("dp", "ctx", None),
            P("dp", "ctx", None),
            P(None, None, ("dp", "ctx"), None, "tensor"),
            P(None, None, "tensor", ("dp", "ctx")),
            P(None, None, ("dp", "ctx"), "tensor"),
            P(None, None, "tensor", ("dp", "ctx")),
            P(None, None, None, ("tensor", "dp", "ctx")),
            P(None, None, ("tensor", "dp", "ctx")),
            P(None, None, None, ("dp", "ctx")),
        ),
        out_specs=(
            P("dp", "ctx", None),
            P("dp", "ctx", None),
            P(None, None, ("dp", "ctx"), None, "tensor"),
            P(None, ("dp", "ctx"), None, "tensor"),
            P(None, None, "tensor", ("dp", "ctx")),
            P(None, "tensor", ("dp", "ctx")),
            P(None, None, ("dp", "ctx"), "tensor"),
            P(None, ("dp", "ctx"), "tensor"),
            P(None, None, "tensor", ("dp", "ctx")),
            P(None, "tensor", ("dp", "ctx")),
            P(None, None, None, ("tensor", "dp", "ctx")),
            P(None, None, ("tensor", "dp", "ctx")),
            P(None, None, ("tensor", "dp", "ctx")),
            P(None, ("tensor", "dp", "ctx")),
            P(None, None, None, ("dp", "ctx")),
            P(None, None, ("dp", "ctx")),
        ),
        check_vma=False,
    )
```

profile of v0, /device:TPU:0, one launch (start us, length us, event | category | flops | bytes accessed | tf_op | source)
XLA Modules:
  0.0 2503.2 jit_solution(2617174048600316897)
XLA Ops:
  18.0 34.0 %all-gather.2 = bf16[1,1,3,512]{2,1,0,3:T(2,128)(2,1)S(1)} all-gather(bf16[1,1,3,64]{2,1,0,3:T(2,128)(2,1)S(1)} %get-tuple-element.142), channel_id=4, replica_groups=mesh['tensor'=4,'dp'=4,'ctx'=2] {'dp','ctx'}, dimensions={3}, use_global_device_ids=true | all-gather | bytes 3456 | tf_op jit(solution)/shard_map/all_gather | solution.py:284
  52.2 21.0 all-gather
  76.0 46.8 %all-gather.33.cloned.1.call-done = bf16[1,1,2048,3,512]{2,4,3,1,0:T(8,128)(2,1)} async-done(((bf16[1,1,256,3,512]{2,4,3,1,0:T(8,128)(2,1)}), bf16[1,1,2048,3,512]{2,4,3,1,0:T(8,128)(2,1)}) %all-gather.33.cloned.1.call-update) | async-done | bytes 6291472 | tf_op jit(solution)/shard_map/all_gather | solution.py:280
  170.4 17.8 all-gather.6
  201.0 111.5 %all-gather.39.cloned.1.call-done = bf16[1,1,2048,2048]{3,2,1,0:T(8,128)(2,1)} async-done(((bf16[1,1,256,2048]{3,2,1,0:T(8,128)(2,1)}), bf16[1,1,2048,2048]{3,2,1,0:T(8,128)(2,1)}) %all-gather.39.cloned.1.call-update) | async-done | bytes 8388624 | tf_op jit(solution)/shard_map/all_gather | solution.py:282
  312.5 17.9 multiply_convert_fusion.3
  330.4 107.7 %all-gather.41.cloned.1.call-done = bf16[1,1,2048,2048]{3,2,1,0:T(8,128)(2,1)} async-done(((bf16[1,1,2048,256]{3,2,1,0:T(8,128)(2,1)}), bf16[1,1,2048,2048]{3,2,1,0:T(8,128)(2,1)}) %all-gather.41.cloned.1.call-update) | async-done | bytes 8388624 | tf_op jit(solution)/shard_map/all_gather | solution.py:283
  438.1 10.5 fusion.10
  448.7 39.9 %all-gather.37.cloned.1.call-done = bf16[1,1,512,2048]{3,2,1,0:T(8,128)(2,1)} async-done(((bf16[1,1,512,256]{3,2,1,0:T(8,128)(2,1)}), bf16[1,1,512,2048]{3,2,1,0:T(8,128)(2,1)}) %all-gather.37.cloned.1.call-update) | async-done | bytes 2097168 | tf_op jit(solution)/shard_map/all_gather | solution.py:281
  496.3 30.7 %all-gather.10 = bf16[1,1,3,512]{2,1,0,3:T(2,128)(2,1)S(1)} all-gather(bf16[1,1,3,64]{2,1,0,3:T(2,128)(2,1)S(1)} %get-tuple-element.141), channel_id=12, replica_groups=mesh['tensor'=4,'dp'=4,'ctx'=2] {'dp','ctx'}, dimensions={3}, use_global_device_ids=true | all-gather | bytes 3456 | tf_op jit(solution)/shard_map/all_gather | solution.py:284
  527.2 18.1 all-gather.8
  545.4 33.2 %all-reduce.7.cloned.1.call-done = f32[1,512,2048]{2,1,0:T(8,128)} async-done(((f32[1,512,2048]{2,1,0:T(8,128)}), f32[1,512,2048]{2,1,0:T(8,128)}) %all-reduce.7.cloned.1.call-update) | async-done | bytes 4194320 | tf_op jit(solution)/shard_map/psum | solution.py:130
  583.9 96.9 %all-gather.43.cloned.1.call-done = bf16[1,1,2048,3,512]{2,4,3,1,0:T(8,128)(2,1)} async-done(((bf16[1,1,256,3,512]{2,4,3,1,0:T(8,128)(2,1)}), bf16[1,1,2048,3,512]{2,4,3,1,0:T(8,128)(2,1)}) %all-gather.43.cloned.1.call-update) | async-done | bytes 6291472 | tf_op jit(solution)/shard_map/all_gather | solution.py:280
  700.9 18.2 all-gather.14
  719.1 12.4 all-gather.47.cloned.1.call-done
  735.5 17.5 all-gather.31.cloned.1.call-done
  760.2 119.9 %all-gather.49.cloned.1.call-done = bf16[1,1,2048,2048]{3,2,1,0:T(8,128)(2,1)} async-done(((bf16[1,1,256,2048]{3,2,1,0:T(8,128)(2,1)}), bf16[1,1,2048,2048]{3,2,1,0:T(8,128)(2,1)}) %all-gather.49.cloned.1.call-update) | async-done | bytes 8388624 | tf_op jit(solution)/shard_map/all_gather | solution.py:282
  880.2 19.1 multiply_convert_fusion.2
  909.8 118.3 %all-gather.51.cloned.1.call-done = bf16[1,1,2048,2048]{3,2,1,0:T(8,128)(2,1)} async-done(((bf16[1,1,2048,256]{3,2,1,0:T(8,128)(2,1)}), bf16[1,1,2048,2048]{3,2,1,0:T(8,128)(2,1)}) %all-gather.51.cloned.1.call-update) | async-done | bytes 8388624 | tf_op jit(solution)/shard_map/all_gather | solution.py:283
  1028.1 10.8 fusion.261
  1051.9 20.0 reduce-scatter.16.cloned.1.call-done
  1097.8 71.1 %all-reduce.13.cloned.1.call-done = (bf16[1,512,2048]{2,1,0:T(8,128)(2,1)}, bf16[1,512,2048]{2,1,0:T(8,128)(2,1)}) async-done(((bf16[1,512,2048]{2,1,0:T(8,128)(2,1)}, bf16[1,512,2048]{2,1,0:T(8,128)(2,1)}), (bf16[1,512,2048]{2,1,0:T(8,128)(2,1)}, bf16[1,512,2048]{2,1,0:T(8,128)(2,1)})) %all-reduce.13.cloned.1.call-update) | async-done | bytes 4194320 | tf_op jit(solution)/shard_map/psum | solution.py:236
  1178.6 78.8 %all-reduce.9.cloned.1.call-done = f32[1,512,2048]{2,1,0:T(8,128)} async-done(((f32[1,512,2048]{2,1,0:T(8,128)}), f32[1,512,2048]{2,1,0:T(8,128)}) %all-reduce.9.cloned.1.call-update) | async-done | bytes 4194320 | tf_op jit(solution)/shard_map/psum | solution.py:130
  1283.9 12.3 fusion.262
  1356.5 68.0 %all-reduce.11.cloned.1.call-done = (bf16[1,512,2048]{2,1,0:T(8,128)(2,1)}, bf16[1,512,2048]{2,1,0:T(8,128)(2,1)}) async-done(((bf16[1,512,2048]{2,1,0:T(8,128)(2,1)}, bf16[1,512,2048]{2,1,0:T(8,128)(2,1)}), (bf16[1,512,2048]{2,1,0:T(8,128)(2,1)}, bf16[1,512,2048]{2,1,0:T(8,128)(2,1)})) %all-reduce.11.cloned.1.call-update) | async-done | bytes 4194320 | tf_op jit(solution)/shard_map/psum | solution.py:235
  1502.3 52.5 %reduce-scatter.34.cloned.1.call-done = bf16[64,6]{1,0:T(8,128)(2,1)} async-done(((bf16[512,6]{1,0:T(8,128)(2,1)}), bf16[64,6]{1,0:T(8,128)(2,1)}) %reduce-scatter.34.cloned.1.call-update) | async-done | bytes 784
  1563.4 48.9 %reduce-scatter.32.cloned.1.call-done = bf16[2,5,256]{2,1,0:T(8,128)(2,1)} async-done(((bf16[2,5,2048]{2,1,0:T(8,128)(2,1)}), bf16[2,5,256]{2,1,0:T(8,128)(2,1)}) %reduce-scatter.32.cloned.1.call-update) | async-done | bytes 5136 | tf_op jit(solution)/shard_map/reduce_scatter | solution.py:345
  1615.0 89.1 %reduce-scatter.26.cloned.1.call-done = bf16[2,512,256]{2,1,0:T(8,128)(2,1)} async-done(((bf16[2,512,2048]{2,1,0:T(8,128)(2,1)}), bf16[2,512,256]{2,1,0:T(8,128)(2,1)}) %reduce-scatter.26.cloned.1.call-update) | async-done | bytes 524304 | tf_op jit(solution)/shard_map/reduce_scatter | solution.py:315
  1710.9 204.9 %reduce-scatter.24.cloned.1.call-done = bf16[2,256,3,512]{3,1,2,0:T(8,128)(2,1)} async-done(((bf16[2,2048,3,512]{3,1,2,0:T(8,128)(2,1)}), bf16[2,256,3,512]{3,1,2,0:T(8,128)(2,1)}) %reduce-scatter.24.cloned.1.call-update) | async-done | bytes 1572880 | tf_op jit(solution)/shard_map/reduce_scatter | solution.py:309
  1928.8 269.4 %reduce-scatter.28.cloned.1.call-done = bf16[2,256,2048]{2,1,0:T(8,128)(2,1)} async-done(((bf16[2,2048,2048]{2,1,0:T(8,128)(2,1)}), bf16[2,256,2048]{2,1,0:T(8,128)(2,1)}) %reduce-scatter.28.cloned.1.call-update) | async-done | bytes 2097168 | tf_op jit(solution)/shard_map/reduce_scatter | solution.py:321
  2209.6 10.1 pad_maximum_fusion.3
  2219.6 261.5 %reduce-scatter.30.cloned.1.call-done = bf16[2,2048,256]{2,1,0:T(8,128)(2,1)} async-done(((bf16[2,2048,2048]{2,1,0:T(8,128)(2,1)}), bf16[2,2048,256]{2,1,0:T(8,128)(2,1)}) %reduce-scatter.30.cloned.1.call-update) | async-done | bytes 2097168 | tf_op jit(solution)/shard_map/reduce_scatter | solution.py:327
  (427 shorter events, 398.2 us)
Async XLA Ops:
  7.2 115.6 %all-gather.33.cloned.1.call-start = ((), (), s32[]{:S(2)}) async-start(), calls=%async_computation.24 | async-start | bytes 7077888 | tf_op jit(solution)/shard_map/all_gather | solution.py:280
  17.7 173.2 %all-gather.29.cloned.1.call-start = ((), (), s32[]{:S(2)}) async-start(), calls=%async_computation.11 | async-start | bytes 1572864 | tf_op jit(solution)/shard_map/all_gather | solution.py:106
  73.6 238.9 %copy-start.63 = (f32[512]{0:T(512)}, f32[512]{0:T(512)S(1)}, u32[]{:S(2)}) copy-start(f32[512]{0:T(512)S(1)} %broadcast_multiply_fusion.1) | copy-start | bytes 6148
  74.9 237.6 %copy-start.69 = (f32[512]{0:T(512)}, f32[512]{0:T(512)S(1)}, u32[]{:S(2)}) copy-start(f32[512]{0:T(512)S(1)} %fusion.221) | copy-start | bytes 6148
  76.0 236.6 %copy-start.59 = (f32[1,1,1,2048]{3,1,2,0:T(1,128)}, f32[1,1,1,2048]{3,1,2,0:T(1,128)S(1)}, u32[]{:S(2)}) copy-start(f32[1,1,1,2048]{3,1,2,0:T(1,128)S(1)} %get-tuple-element.150) | copy-start | bytes 24580
  142.3 54.8 %all-gather.35.cloned.1.call-start = ((), (), s32[]{:S(2)}) async-start(), calls=%async_computation.25 | async-start | bytes 1572864 | tf_op jit(solution)/shard_map/all_gather | solution.py:107
  144.5 168.1 %all-gather.39.cloned.1.call-start = ((), (), s32[]{:S(2)}) async-start(), calls=%async_computation.27 | async-start | bytes 9437184 | tf_op jit(solution)/shard_map/all_gather | solution.py:282
  156.4 281.7 %all-gather.41.cloned.1.call-start = ((), (), s32[]{:S(2)}) async-start(), calls=%async_computation.28 | async-start | bytes 9437184 | tf_op jit(solution)/shard_map/all_gather | solution.py:283
  167.4 321.2 %all-gather.37.cloned.1.call-start = ((), (), s32[]{:S(2)}) async-start(), calls=%async_computation.26 | async-start | bytes 2359296 | tf_op jit(solution)/shard_map/all_gather | solution.py:281
  170.3 408.2 %all-reduce.7.cloned.1.call-start = ((), (), s32[]{:S(2)}) async-start(), calls=%async_computation.12 | async-start | bytes 8388608 | tf_op jit(solution)/shard_map/psum | solution.py:130
  201.0 287.6 %copy-start.37 = (bf16[2,256,512]{2,1,0:T(8,128)(2,1)}, bf16[2,256,512]{2,1,0:T(8,128)(2,1)S(1)}, u32[]{:S(2)}) copy-start(bf16[2,256,512]{2,1,0:T(8,128)(2,1)S(1)} %fusion.177) | copy-start | bytes 1572868
  494.7 186.1 %all-gather.43.cloned.1.call-start = ((), (), s32[]{:S(2)}) async-start(), calls=%async_computation.29 | async-start | bytes 7077888 | tf_op jit(solution)/shard_map/all_gather | solution.py:280
  495.5 236.0 %all-gather.47.cloned.1.call-start = ((), (), s32[]{:S(2)}) async-start(), calls=%async_computation.31 | async-start | bytes 2359296 | tf_op jit(solution)/shard_map/all_gather | solution.py:281
  496.2 256.7 %all-gather.31.cloned.1.call-start = ((), (), s32[]{:S(2)}) async-start(), calls=%async_computation.13 | async-start | bytes 1572864 | tf_op jit(solution)/shard_map/all_gather | solution.py:106
  545.3 334.8 %copy-start.81 = (f32[1,1,1,2048]{3,1,2,0:T(1,128)}, f32[1,1,1,2048]{3,1,2,0:T(1,128)S(1)}, u32[]{:S(2)}) copy-start(f32[1,1,1,2048]{3,1,2,0:T(1,128)S(1)} %get-tuple-element.147) | copy-start | bytes 24580
  697.2 183.0 %all-gather.49.cloned.1.call-start = ((), (), s32[]{:S(2)}) async-start(), calls=%async_computation.32 | async-start | bytes 9437184 | tf_op jit(solution)/shard_map/all_gather | solution.py:282
  697.9 203.2 %all-gather.45.cloned.1.call-start = ((), (), s32[]{:S(2)}) async-start(), calls=%async_computation.30 | async-start | bytes 1572864 | tf_op jit(solution)/shard_map/all_gather | solution.py:107
  700.1 328.0 %all-gather.51.cloned.1.call-start = ((), (), s32[]{:S(2)}) async-start(), calls=%async_computation.33 | async-start | bytes 9437184 | tf_op jit(solution)/shard_map/all_gather | solution.py:283
  700.8 349.0 %reduce-scatter.18.cloned.1.call-start = ((), (), s32[]{:S(2)}) async-start(), calls=%async_computation.16 | async-start | bytes 1572864 | tf_op jit(solution)/shard_map/reduce_scatter | solution.py:212
  759.8 312.1 %reduce-scatter.16.cloned.1.call-start = ((), (), s32[]{:S(2)}) async-start(), calls=%async_computation.15 | async-start | bytes 1572864 | tf_op jit(solution)/shard_map/reduce_scatter | solution.py:209
  909.5 259.3 %all-reduce.13.cloned.1.call-start = ((), (), s32[]{:S(2)}) async-start(), calls=%async_computation.37 | async-start | bytes 8388608 | tf_op jit(solution)/shard_map/psum | solution.py:236
  1083.2 174.1 %all-reduce.9.cloned.1.call-start = ((), (), s32[]{:S(2)}) async-start(), calls=%async_computation.14 | async-start | bytes 8388608 | tf_op jit(solution)/shard_map/psum | solution.py:130
  1097.1 209.6 %reduce-scatter.22.cloned.1.call-start = ((), (), s32[]{:S(2)}) async-start(), calls=%async_computation.18 | async-start | bytes 1572864 | tf_op jit(solution)/shard_map/reduce_scatter | solution.py:212
  1273.0 43.9 %reduce-scatter.20.cloned.1.call-start = ((), (), s32[]{:S(2)}) async-start(), calls=%async_computation.17 | async-start | bytes 1572864 | tf_op jit(solution)/shard_map/reduce_scatter | solution.py:209
  1283.8 140.7 %all-reduce.11.cloned.1.call-start = ((), (), s32[]{:S(2)}) async-start(), calls=%async_computation.36 | async-start | bytes 8388608 | tf_op jit(solution)/shard_map/psum | solution.py:235
  1338.8 161.3 %reduce-scatter.36.cloned.1.call-start = ((), (), s32[]{:S(2)}) async-start(), calls=%async_computation.35 | async-start | bytes 589824
  1353.6 201.2 %reduce-scatter.34.cloned.1.call-start = ((), (), s32[]{:S(2)}) async-start(), calls=%async_computation.34 | async-start | bytes 147456
  1356.2 256.1 %reduce-scatter.32.cloned.1.call-start = ((), (), s32[]{:S(2)}) async-start(), calls=%async_computation.23 | async-start | bytes 73728 | tf_op jit(solution)/shard_map/reduce_scatter | solution.py:345
  1438.4 265.8 %reduce-scatter.26.cloned.1.call-start = ((), (), s32[]{:S(2)}) async-start(), calls=%async_computation.20 | async-start | bytes 4718592 | tf_op jit(solution)/shard_map/reduce_scatter | solution.py:315
  1443.1 472.8 %reduce-scatter.24.cloned.1.call-start = ((), (), s32[]{:S(2)}) async-start(), calls=%async_computation.19 | async-start | bytes 14155776 | tf_op jit(solution)/shard_map/reduce_scatter | solution.py:309
  1460.1 738.1 %reduce-scatter.28.cloned.1.call-start = ((), (), s32[]{:S(2)}) async-start(), calls=%async_computation.21 | async-start | bytes 18874368 | tf_op jit(solution)/shard_map/reduce_scatter | solution.py:321
  1480.6 1000.5 %reduce-scatter.30.cloned.1.call-start = ((), (), s32[]{:S(2)}) async-start(), calls=%async_computation.22 | async-start | bytes 18874368 | tf_op jit(solution)/shard_map/reduce_scatter | solution.py:327
  (87 other events, 1357.0 us)
Sparse Core Ops, SparseCore 0:
  17.8 104.9 all-gather.32
  142.4 19.4 all-gather.28
  164.0 21.3 all-gather.34
  188.0 124.4 all-gather.38
  315.0 123.1 all-gather.40
  440.0 48.4 all-gather.36
  494.8 83.6 all-reduce.6
  581.2 99.6 all-gather.42
  682.9 48.5 all-gather.46
  733.5 19.4 all-gather.30
  755.7 124.4 all-gather.48
  881.6 19.4 all-gather.44
  903.1 124.9 all-gather.50
  1030.2 18.5 reduce-scatter.17
  1051.4 20.3 reduce-scatter.15
  1083.4 85.4 all-reduce.12
  1171.7 85.6 all-reduce.8
  1273.1 20.5 reduce-scatter.21
  1296.5 20.3 reduce-scatter.19
  1338.9 85.4 all-reduce.10
  1427.8 62.7 reduce-scatter.35
  1493.9 60.8 reduce-scatter.33
  1558.5 53.7 reduce-scatter.31
  1616.4 87.7 reduce-scatter.25
  1708.3 207.4 reduce-scatter.23
  1919.5 278.6 reduce-scatter.27
  2201.8 279.2 reduce-scatter.29
where the time goes:
time: 2510 us; the launch traced here: 2500 us
  waiting for transfers between devices  1880 us (75%)
  matrix products  212 us (8%)
  other arithmetic  172 us (7%)
  blocking collectives  140 us (6%)
  local copies, waits for them, and re-layouts  78.9 us (3%)
    reduce_scatter x1, waiting for transfers between devices, local(): lax.psum_scatter(stack_member(collected, 2).astype(jnp.bfloat16), ('dp',...  269 us
    reduce_scatter x1, waiting for transfers between devices, local(): lax.psum_scatter(stack_member(collected, 3).astype(jnp.bfloat16), ('dp',...  261 us
    all_gather x2, waiting for transfers between devices, local(): lax.all_gather(lowered(up_state, layer_index), ('dp', 'ctx'), axis=0, til...  231 us
    all_gather x2, waiting for transfers between devices, local(): lax.all_gather(lowered(down_state, layer_index), ('dp', 'ctx'), axis=1, t...  226 us
    reduce_scatter x1, waiting for transfers between devices, local(): lax.psum_scatter(stack_member(collected, 0).astype(jnp.bfloat16), ('dp',...  205 us
    all_gather x2, waiting for transfers between devices, local(): lax.all_gather(lowered(qkv_state, layer_index), ('dp', 'ctx'), axis=0, ti...  144 us
    psum x2, waiting for transfers between devices, forward_layer(): branch = lax.psum(summand, 'tensor')  112 us
    reduce_scatter x1, waiting for transfers between devices, local(): lax.psum_scatter(stack_member(collected, 1).astype(jnp.bfloat16), ('dp',...  89.1 us
  transfers between devices with their start and end apart: 27, of which 22 were waited for; matrix products, arithmetic and copies ran while one was open for 14% of the time, Pallas kernels for 0%

commit v1 on v0

--- a/solution.py
+++ b/solution.py
@@ -127,7 +127,9 @@
     summand = summand + jnp.einsum(
         "scf,fd->scd", activation, down_weight, preferred_element_type=jnp.float32
     )
-    branch = lax.psum(summand, "tensor")
+    branch = summand
+    for hop in (1, 2):
+        branch = branch + lax.ppermute(branch, "tensor", [(dev, dev ^ hop) for dev in range(4)])
     saved = (
         hidden,
         normed_one,

time: 2510 us -> 2420 us (0.964)
  waiting for transfers between devices: 1880 us -> 1760 us
    psum x2 -> x0, waiting for transfers between devices: 112 us -> none  [forward_layer(): branch = lax.psum(summand, 'tensor')]
    all_gather x2, waiting for transfers between devices: 144 us -> 46.8 us  [local(): lax.all_gather(lowered(qkv_state, layer_index), ('dp', 'ctx'), axis=0, ti...]
    psum x1, waiting for transfers between devices: 71.1 us -> 151 us  [backward_layer(): lax.psum(grad_normed_two.astype(jnp.bfloat16), 'tensor').astype(jnp.float32)]
    ppermute x0 -> x4, waiting for transfers between devices: none -> 37.8 us  [forward_layer(): lax.ppermute(branch, 'tensor', [(dev, dev ^ hop) for dev in range(4)])]
    unnamed x29 -> x27, waiting for transfers between devices: 55.6 us -> 55.1 us
  transfers between devices with their start and end apart: 27 -> 29, of which waited for: 22 -> 21; matrix products, arithmetic and copies ran while one was open for 14% -> 16% of each run, Pallas kernels for 0% -> 0%
where the time goes in v1:
time: 2420 us; the launch traced here: 2410 us
  waiting for transfers between devices  1760 us (73%)
  matrix products  215 us (9%)
  other arithmetic  182 us (8%)
  blocking collectives  152 us (6%)
  local copies, waits for them, and re-layouts  81 us (3%)
    reduce_scatter x1, waiting for transfers between devices, local(): lax.psum_scatter(stack_member(collected, 2).astype(jnp.bfloat16), ('dp',...  269 us
    reduce_scatter x1, waiting for transfers between devices, local(): lax.psum_scatter(stack_member(collected, 3).astype(jnp.bfloat16), ('dp',...  262 us
    all_gather x2, waiting for transfers between devices, local(): lax.all_gather(lowered(up_state, layer_index), ('dp', 'ctx'), axis=0, til...  227 us
    all_gather x2, waiting for transfers between devices, local(): lax.all_gather(lowered(down_state, layer_index), ('dp', 'ctx'), axis=1, t...  213 us
    reduce_scatter x1, waiting for transfers between devices, local(): lax.psum_scatter(stack_member(collected, 0).astype(jnp.bfloat16), ('dp',...  205 us
    psum x1, waiting for transfers between devices, backward_layer(): lax.psum(grad_normed_two.astype(jnp.bfloat16), 'tensor').astype(jnp.float32)  151 us
    reduce_scatter x1, waiting for transfers between devices, local(): lax.psum_scatter(stack_member(collected, 1).astype(jnp.bfloat16), ('dp',...  89.3 us
    psum x1, waiting for transfers between devices, backward_layer(): lax.psum(grad_normed_one.astype(jnp.bfloat16), 'tensor').astype(jnp.float32)  68 us
  transfers between devices with their start and end apart: 29, of which 21 were waited for; matrix products, arithmetic and copies ran while one was open for 16% of the time, Pallas kernels for 0%

profile of v1, /device:TPU:0, one launch (start us, length us, event | category | flops | bytes accessed | tf_op | source)
XLA Modules:
  0.0 2410.4 jit_solution(14158617863019300396)
XLA Ops:
  18.0 34.0 %all-gather.2 = bf16[1,1,3,512]{2,1,0,3:T(2,128)(2,1)S(1)} all-gather(bf16[1,1,3,64]{2,1,0,3:T(2,128)(2,1)S(1)} %get-tuple-element.142), channel_id=4, replica_groups=mesh['tensor'=4,'dp'=4,'ctx'=2] {'dp','ctx'}, dimensions={3}, use_global_device_ids=true | all-gather | bytes 3456 | tf_op jit(solution)/shard_map/all_gather | solution.py:286
  52.2 21.0 all-gather
  76.0 46.8 %all-gather.33.cloned.1.call-done = bf16[1,1,2048,3,512]{2,4,3,1,0:T(8,128)(2,1)} async-done(((bf16[1,1,256,3,512]{2,4,3,1,0:T(8,128)(2,1)}), bf16[1,1,2048,3,512]{2,4,3,1,0:T(8,128)(2,1)}) %all-gather.33.cloned.1.call-update) | async-done | bytes 6291472 | tf_op jit(solution)/shard_map/all_gather | solution.py:282
  173.3 18.0 all-gather.6
  203.9 108.7 %all-gather.39.cloned.1.call-done = bf16[1,1,2048,2048]{3,2,1,0:T(8,128)(2,1)} async-done(((bf16[1,1,256,2048]{3,2,1,0:T(8,128)(2,1)}), bf16[1,1,2048,2048]{3,2,1,0:T(8,128)(2,1)}) %all-gather.39.cloned.1.call-update) | async-done | bytes 8388624 | tf_op jit(solution)/shard_map/all_gather | solution.py:284
  312.6 17.9 multiply_convert_fusion.3
  330.4 107.7 %all-gather.41.cloned.1.call-done = bf16[1,1,2048,2048]{3,2,1,0:T(8,128)(2,1)} async-done(((bf16[1,1,2048,256]{3,2,1,0:T(8,128)(2,1)}), bf16[1,1,2048,2048]{3,2,1,0:T(8,128)(2,1)}) %all-gather.41.cloned.1.call-update) | async-done | bytes 8388624 | tf_op jit(solution)/shard_map/all_gather | solution.py:285
  438.2 10.5 fusion.10
  448.7 40.5 %all-gather.37.cloned.1.call-done = bf16[1,1,512,2048]{3,2,1,0:T(8,128)(2,1)} async-done(((bf16[1,1,512,256]{3,2,1,0:T(8,128)(2,1)}), bf16[1,1,512,2048]{3,2,1,0:T(8,128)(2,1)}) %all-gather.37.cloned.1.call-update) | async-done | bytes 2097168 | tf_op jit(solution)/shard_map/all_gather | solution.py:283
  504.9 32.1 %all-gather.10 = bf16[1,1,3,512]{2,1,0,3:T(2,128)(2,1)S(1)} all-gather(bf16[1,1,3,64]{2,1,0,3:T(2,128)(2,1)S(1)} %get-tuple-element.141), channel_id=12, replica_groups=mesh['tensor'=4,'dp'=4,'ctx'=2] {'dp','ctx'}, dimensions={3}, use_global_device_ids=true | all-gather | bytes 3456 | tf_op jit(solution)/shard_map/all_gather | solution.py:286
  537.1 28.5 %all-gather.8 = bf16[1,1,5,2048]{3,1,2,0:T(2,128)(2,1)S(1)} all-gather(bf16[1,1,5,256]{3,1,2,0:T(2,128)(2,1)S(1)} %get-tuple-element.159), channel_id=10, replica_groups=mesh['tensor'=4,'dp'=4,'ctx'=2] {'dp','ctx'}, dimensions={3}, use_global_device_ids=true | all-gather | bytes 23040 | tf_op jit(solution)/shard_map/all_gather | solution.py:288
  565.7 30.7 %collective-permute-done.1 = f32[1,512,2048]{2,1,0:T(8,128)} collective-permute-done((f32[1,512,2048]{2,1,0:T(8,128)}, f32[1,512,2048]{2,1,0:T(8,128)}, u32[]{:S(2)}, u32[]{:S(2)}) %collective-permute-start.1) | collective-permute-done | bytes 4194336 | tf_op jit(solution)/shard_map/ppermute | solution.py:132
  620.6 18.4 all-gather.14
  650.9 118.1 %all-gather.49.cloned.1.call-done = bf16[1,1,2048,2048]{3,2,1,0:T(8,128)(2,1)} async-done(((bf16[1,1,256,2048]{3,2,1,0:T(8,128)(2,1)}), bf16[1,1,2048,2048]{3,2,1,0:T(8,128)(2,1)}) %all-gather.49.cloned.1.call-update) | async-done | bytes 8388624 | tf_op jit(solution)/shard_map/all_gather | solution.py:284
  769.0 19.3 multiply_convert_fusion.2
  788.3 105.7 %all-gather.51.cloned.1.call-done = bf16[1,1,2048,2048]{3,2,1,0:T(8,128)(2,1)} async-done(((bf16[1,1,2048,256]{3,2,1,0:T(8,128)(2,1)}), bf16[1,1,2048,2048]{3,2,1,0:T(8,128)(2,1)}) %all-gather.51.cloned.1.call-update) | async-done | bytes 8388624 | tf_op jit(solution)/shard_map/all_gather | solution.py:285
  894.0 10.5 fusion.2
  904.5 11.2 all-gather.31.cloned.1.call-done
  922.5 15.8 all-gather.45.cloned.1.call-done
  952.1 11.4 fusion.261
  963.5 9.9 fusion.96
  1005.1 150.6 %all-reduce.7.cloned.1.call-done = (bf16[1,512,2048]{2,1,0:T(8,128)(2,1)}, bf16[1,512,2048]{2,1,0:T(8,128)(2,1)}) async-done(((bf16[1,512,2048]{2,1,0:T(8,128)(2,1)}, bf16[1,512,2048]{2,1,0:T(8,128)(2,1)}), (bf16[1,512,2048]{2,1,0:T(8,128)(2,1)}, bf16[1,512,2048]{2,1,0:T(8,128)(2,1)})) %all-reduce.7.cloned.1.call-update) | async-done | bytes 4194320 | tf_op jit(solution)/shard_map/psum | solution.py:238
  1191.2 12.5 fusion.262
  1263.9 68.0 %all-reduce.5.cloned.1.call-done = (bf16[1,512,2048]{2,1,0:T(8,128)(2,1)}, bf16[1,512,2048]{2,1,0:T(8,128)(2,1)}) async-done(((bf16[1,512,2048]{2,1,0:T(8,128)(2,1)}, bf16[1,512,2048]{2,1,0:T(8,128)(2,1)}), (bf16[1,512,2048]{2,1,0:T(8,128)(2,1)}, bf16[1,512,2048]{2,1,0:T(8,128)(2,1)})) %all-reduce.5.cloned.1.call-update) | async-done | bytes 4194320 | tf_op jit(solution)/shard_map/psum | solution.py:237
  1410.0 52.1 %reduce-scatter.34.cloned.1.call-done = bf16[64,6]{1,0:T(8,128)(2,1)} async-done(((bf16[512,6]{1,0:T(8,128)(2,1)}), bf16[64,6]{1,0:T(8,128)(2,1)}) %reduce-scatter.34.cloned.1.call-update) | async-done | bytes 784
  1470.7 48.9 %reduce-scatter.32.cloned.1.call-done = bf16[2,5,256]{2,1,0:T(8,128)(2,1)} async-done(((bf16[2,5,2048]{2,1,0:T(8,128)(2,1)}), bf16[2,5,256]{2,1,0:T(8,128)(2,1)}) %reduce-scatter.32.cloned.1.call-update) | async-done | bytes 5136 | tf_op jit(solution)/shard_map/reduce_scatter | solution.py:347
  1522.3 89.3 %reduce-scatter.26.cloned.1.call-done = bf16[2,512,256]{2,1,0:T(8,128)(2,1)} async-done(((bf16[2,512,2048]{2,1,0:T(8,128)(2,1)}), bf16[2,512,256]{2,1,0:T(8,128)(2,1)}) %reduce-scatter.26.cloned.1.call-update) | async-done | bytes 524304 | tf_op jit(solution)/shard_map/reduce_scatter | solution.py:317
  1618.4 204.9 %reduce-scatter.24.cloned.1.call-done = bf16[2,256,3,512]{3,1,2,0:T(8,128)(2,1)} async-done(((bf16[2,2048,3,512]{3,1,2,0:T(8,128)(2,1)}), bf16[2,256,3,512]{3,1,2,0:T(8,128)(2,1)}) %reduce-scatter.24.cloned.1.call-update) | async-done | bytes 1572880 | tf_op jit(solution)/shard_map/reduce_scatter | solution.py:311
  1836.2 269.4 %reduce-scatter.28.cloned.1.call-done = bf16[2,256,2048]{2,1,0:T(8,128)(2,1)} async-done(((bf16[2,2048,2048]{2,1,0:T(8,128)(2,1)}), bf16[2,256,2048]{2,1,0:T(8,128)(2,1)}) %reduce-scatter.28.cloned.1.call-update) | async-done | bytes 2097168 | tf_op jit(solution)/shard_map/reduce_scatter | solution.py:323
  2117.0 10.1 pad_maximum_fusion.3
  2127.1 261.6 %reduce-scatter.30.cloned.1.call-done = bf16[2,2048,256]{2,1,0:T(8,128)(2,1)} async-done(((bf16[2,2048,2048]{2,1,0:T(8,128)(2,1)}), bf16[2,2048,256]{2,1,0:T(8,128)(2,1)}) %reduce-scatter.30.cloned.1.call-update) | async-done | bytes 2097168 | tf_op jit(solution)/shard_map/reduce_scatter | solution.py:329
  2388.7 9.6 fusion.62
  (427 shorter events, 401.2 us)
Async XLA Ops:
  7.2 115.6 %all-gather.33.cloned.1.call-start = ((), (), s32[]{:S(2)}) async-start(), calls=%async_computation.22 | async-start | bytes 7077888 | tf_op jit(solution)/shard_map/all_gather | solution.py:282
  17.7 176.3 %all-gather.29.cloned.1.call-start = ((), (), s32[]{:S(2)}) async-start(), calls=%async_computation.11 | async-start | bytes 1572864 | tf_op jit(solution)/shard_map/all_gather | solution.py:106
  73.6 238.9 %copy-start.62 = (f32[512]{0:T(512)}, f32[512]{0:T(512)S(1)}, u32[]{:S(2)}) copy-start(f32[512]{0:T(512)S(1)} %broadcast_multiply_fusion.1) | copy-start | bytes 6148
  74.9 237.7 %copy-start.68 = (f32[512]{0:T(512)}, f32[512]{0:T(512)S(1)}, u32[]{:S(2)}) copy-start(f32[512]{0:T(512)S(1)} %fusion.221) | copy-start | bytes 6148
  142.3 58.0 %all-gather.35.cloned.1.call-start = ((), (), s32[]{:S(2)}) async-start(), calls=%async_computation.23 | async-start | bytes 1572864 | tf_op jit(solution)/shard_map/all_gather | solution.py:107
  144.5 168.1 %all-gather.39.cloned.1.call-start = ((), (), s32[]{:S(2)}) async-start(), calls=%async_computation.25 | async-start | bytes 9437184 | tf_op jit(solution)/shard_map/all_gather | solution.py:284
  156.4 281.7 %all-gather.41.cloned.1.call-start = ((), (), s32[]{:S(2)}) async-start(), calls=%async_computation.26 | async-start | bytes 9437184 | tf_op jit(solution)/shard_map/all_gather | solution.py:285
  167.4 321.8 %all-gather.37.cloned.1.call-start = ((), (), s32[]{:S(2)}) async-start(), calls=%async_computation.24 | async-start | bytes 2359296 | tf_op jit(solution)/shard_map/all_gather | solution.py:283
  170.4 432.8 %all-gather.43.cloned.1.call-start = ((), (), s32[]{:S(2)}) async-start(), calls=%async_computation.27 | async-start | bytes 7077888 | tf_op jit(solution)/shard_map/all_gather | solution.py:282
  171.1 472.5 %all-gather.47.cloned.1.call-start = ((), (), s32[]{:S(2)}) async-start(), calls=%async_computation.29 | async-start | bytes 2359296 | tf_op jit(solution)/shard_map/all_gather | solution.py:283
  171.9 597.1 %all-gather.49.cloned.1.call-start = ((), (), s32[]{:S(2)}) async-start(), calls=%async_computation.30 | async-start | bytes 9437184 | tf_op jit(solution)/shard_map/all_gather | solution.py:284
  172.6 721.4 %all-gather.51.cloned.1.call-start = ((), (), s32[]{:S(2)}) async-start(), calls=%async_computation.31 | async-start | bytes 9437184 | tf_op jit(solution)/shard_map/all_gather | solution.py:285
  173.2 742.5 %all-gather.31.cloned.1.call-start = ((), (), s32[]{:S(2)}) async-start(), calls=%async_computation.12 | async-start | bytes 1572864 | tf_op jit(solution)/shard_map/all_gather | solution.py:106
  203.9 285.3 %copy-start.36 = (bf16[2,256,512]{2,1,0:T(8,128)(2,1)}, bf16[2,256,512]{2,1,0:T(8,128)(2,1)S(1)}, u32[]{:S(2)}) copy-start(bf16[2,256,512]{2,1,0:T(8,128)(2,1)S(1)} %fusion.177) | copy-start | bytes 1572868
  493.4 7.2 collective-permute-start
  503.4 92.9 %collective-permute-start.1 = (f32[1,512,2048]{2,1,0:T(8,128)}, f32[1,512,2048]{2,1,0:T(8,128)}, u32[]{:S(2)}, u32[]{:S(2)}) collective-permute-start(f32[1,512,2048]{2,1,0:T(8,128)} %add.364), channel_id=1, source_target_pairs={{0,16},{8,24},{16,0},{24,8},{1,17},{9,25},{17,1},{25,9},{2,18},{10... | collective-permute-start | bytes 12582920 | tf_op jit(solution)/shard_map/ppermute | solution.py:132
  620.6 317.8 %all-gather.45.cloned.1.call-start = ((), (), s32[]{:S(2)}) async-start(), calls=%async_computation.28 | async-start | bytes 1572864 | tf_op jit(solution)/shard_map/all_gather | solution.py:107
  650.9 323.5 %reduce-scatter.18.cloned.1.call-start = ((), (), s32[]{:S(2)}) async-start(), calls=%async_computation.14 | async-start | bytes 1572864 | tf_op jit(solution)/shard_map/reduce_scatter | solution.py:214
  922.5 61.6 %reduce-scatter.16.cloned.1.call-start = ((), (), s32[]{:S(2)}) async-start(), calls=%async_computation.13 | async-start | bytes 1572864 | tf_op jit(solution)/shard_map/reduce_scatter | solution.py:211
  946.1 42.8 %collective-permute-start.2 = (f32[1,512,2048]{2,1,0:T(8,128)}, f32[1,512,2048]{2,1,0:T(8,128)}, u32[]{:S(2)}, u32[]{:S(2)}) collective-permute-start(f32[1,512,2048]{2,1,0:T(8,128)} %add_bitcast_fusion), channel_id=1, source_target_pairs={{0,8},{8,0},{16,24},{24,16},{1,9},{9,1},{17,25},{25,17},{2,10},{10... | collective-permute-start | bytes 12582920 | tf_op jit(solution)/shard_map/ppermute | solution.py:132
  952.1 203.6 %all-reduce.7.cloned.1.call-start = ((), (), s32[]{:S(2)}) async-start(), calls=%async_computation.35 | async-start | bytes 8388608 | tf_op jit(solution)/shard_map/psum | solution.py:238
  995.6 169.8 %collective-permute-start.3 = (f32[1,512,2048]{2,1,0:T(8,128)}, f32[1,512,2048]{2,1,0:T(8,128)}, u32[]{:S(2)}, u32[]{:S(2)}) collective-permute-start(f32[1,512,2048]{2,1,0:T(8,128)} %add.385), channel_id=1, source_target_pairs={{0,16},{8,24},{16,0},{24,8},{1,17},{9,25},{17,1},{25,9},{2,18},{10... | collective-permute-start | bytes 12582920 | tf_op jit(solution)/shard_map/ppermute | solution.py:132
  1004.4 210.1 %reduce-scatter.22.cloned.1.call-start = ((), (), s32[]{:S(2)}) async-start(), calls=%async_computation.16 | async-start | bytes 1572864 | tf_op jit(solution)/shard_map/reduce_scatter | solution.py:214
  1180.7 43.6 %reduce-scatter.20.cloned.1.call-start = ((), (), s32[]{:S(2)}) async-start(), calls=%async_computation.15 | async-start | bytes 1572864 | tf_op jit(solution)/shard_map/reduce_scatter | solution.py:211
  1191.2 140.7 %all-reduce.5.cloned.1.call-start = ((), (), s32[]{:S(2)}) async-start(), calls=%async_computation.34 | async-start | bytes 8388608 | tf_op jit(solution)/shard_map/psum | solution.py:237
  1246.2 161.6 %reduce-scatter.36.cloned.1.call-start = ((), (), s32[]{:S(2)}) async-start(), calls=%async_computation.33 | async-start | bytes 589824
  1261.1 201.0 %reduce-scatter.34.cloned.1.call-start = ((), (), s32[]{:S(2)}) async-start(), calls=%async_computation.32 | async-start | bytes 147456
  1263.7 255.9 %reduce-scatter.32.cloned.1.call-start = ((), (), s32[]{:S(2)}) async-start(), calls=%async_computation.21 | async-start | bytes 73728 | tf_op jit(solution)/shard_map/reduce_scatter | solution.py:347
  1345.8 265.8 %reduce-scatter.26.cloned.1.call-start = ((), (), s32[]{:S(2)}) async-start(), calls=%async_computation.18 | async-start | bytes 4718592 | tf_op jit(solution)/shard_map/reduce_scatter | solution.py:317
  1350.5 472.8 %reduce-scatter.24.cloned.1.call-start = ((), (), s32[]{:S(2)}) async-start(), calls=%async_computation.17 | async-start | bytes 14155776 | tf_op jit(solution)/shard_map/reduce_scatter | solution.py:311
  1367.5 738.1 %reduce-scatter.28.cloned.1.call-start = ((), (), s32[]{:S(2)}) async-start(), calls=%async_computation.19 | async-start | bytes 18874368 | tf_op jit(solution)/shard_map/reduce_scatter | solution.py:323
  1388.1 1000.7 %reduce-scatter.30.cloned.1.call-start = ((), (), s32[]{:S(2)}) async-start(), calls=%async_computation.20 | async-start | bytes 18874368 | tf_op jit(solution)/shard_map/reduce_scatter | solution.py:329
  (87 other events, 1693.9 us)
Sparse Core Ops, SparseCore 0:
  17.8 104.9 all-gather.32
  142.4 19.4 all-gather.28
  164.1 21.3 all-gather.34
  188.0 124.4 all-gather.38
  315.0 123.1 all-gather.40
  440.6 48.5 all-gather.36
  491.8 100.9 all-gather.42
  594.9 48.6 all-gather.46
  646.3 122.6 all-gather.48
  770.9 123.1 all-gather.50
  896.1 19.4 all-gather.30
  917.0 21.2 all-gather.44
  941.2 20.3 reduce-scatter.17
  963.7 20.3 reduce-scatter.15
  1004.6 151.0 all-reduce.6
  1180.9 20.3 reduce-scatter.21
  1203.9 20.3 reduce-scatter.19
  1246.4 85.4 all-reduce.4
  1335.2 62.7 reduce-scatter.35
  1401.2 60.8 reduce-scatter.33
  1465.8 53.7 reduce-scatter.31
  1523.8 87.7 reduce-scatter.25
  1615.8 207.4 reduce-scatter.23
  1826.9 278.6 reduce-scatter.27
  2109.4 279.2 reduce-scatter.29
